TPU v7x, 32 devices: a whole 2x2x4 slice. The times are simulated.
32 devices in a mesh: row: 4 (over y, x), col: 8 (over z, core).
Axes of the slice: x: 2, y: 2, z: 4, core: 2. Of those that a mesh axis runs over, the one named last changes fastest.
Arguments:
- wrapped: float32 [1, 4096, 8192], P(None, 'row', 'col'), may hold values from -2.8 to 2.8
- col_steps: int32 [1, 4, 8], P(None, 'row', 'col'), may hold values from -2 to 2, as said below
- row_steps: int32 [1, 4, 8], P(None, 'row', 'col'), may hold values from -2 to 2, as said below
Outputs:
- unwrapped: float32 [1, 4096, 8192], P(None, 'row', 'col')
Inputs may be any that keep to these rules, and one draw needn't show every extreme that they name: `col_steps`: nonzero whole numbers; the last tile column has no edge. `row_steps`: nonzero whole numbers; the last tile row has no edge.
All inputs are finite; a program needn't handle non-finite values.
Results may differ from a plain program's by a relative error of at most 0.0003.
Values sent between devices are 32-bit elements; how exact they have to be, the bound alone decides.
No kernel may reach another device: no remote copies, remote signals or barrier semaphores. Data moves between devices by JAX's collectives and lax.ppermute only.
A program may use at most 64 MiB of HBM per device.

v0:
```python
import math

import jax
import jax.numpy as jnp
from jax import lax
from jax.sharding import PartitionSpec as P

ITERS = 2


TWO_PI = 2.0 * math.pi


def extended(cells, sides, width):
    for axis, dim in sides:
        count = lax.axis_size(axis)
        ends = count - 1
        head = lax.slice_in_dim(cells, 0, width, axis=dim)
        tail = lax.slice_in_dim(cells, cells.shape[dim] - width, cells.shape[dim], axis=dim)
        cells = jnp.concatenate(
            [
                lax.ppermute(tail, axis, [(i, (i + 1) % count) for i in range(ends)]),
                cells,
                lax.ppermute(head, axis, [((i + 1) % count, i) for i in range(ends)]),
            ],
            axis=dim,
        )
    return cells


def wrap_diff(change):
    return change - TWO_PI * jnp.floor(change / TWO_PI + 0.5)


def running_sum(values):
    frames, tile_rows, tile_width = values.shape
    block_len = math.gcd(tile_width, 128)
    blocks_in = tile_width // block_len
    pieces = values.reshape(frames, tile_rows, blocks_in, block_len)
    strict_upper = (
        lax.broadcasted_iota(jnp.int32, (block_len, block_len), 0)
        < lax.broadcasted_iota(jnp.int32, (block_len, block_len), 1)
    ).astype(jnp.float32)
    inside = jnp.einsum("frcm,mk->frck", pieces, strict_upper, precision=lax.Precision.HIGHEST)
    totals = jnp.sum(pieces, axis=3)
    before = jnp.cumsum(totals, axis=2) - totals
    return (inside + before[:, :, :, None]).reshape(frames, tile_rows, tile_width)


def integrate_line(line):
    steps = wrap_diff(line[:, 1:] - line[:, :-1])
    running = jnp.cumsum(steps, axis=1)
    return line[:, 0:1] + jnp.concatenate([jnp.zeros_like(line[:, 0:1]), running], axis=1)


def mean_jump(own_edge, crossing, beyond, weights):
    return jnp.sum(weights * (own_edge + crossing - beyond), axis=1) / jnp.sum(weights, axis=1)


def on_device(wrapped, col_steps, row_steps):
    frames, tile_rows, tile_cols = wrapped.shape
    padded = extended(wrapped, (("row", 1), ("col", 2)), 1)
    step_x = wrap_diff(padded[:, :, 1:] - padded[:, :, :-1])
    step_y = wrap_diff(padded[:, 1:, :] - padded[:, :-1, :])
    charge_across = (
        step_x[:, 0:tile_rows, tile_cols - 1]
        + step_y[:, 0:tile_rows, tile_cols]
        - step_x[:, 1 : tile_rows + 1, tile_cols - 1]
        - step_y[:, 0:tile_rows, tile_cols - 1]
    ) / TWO_PI
    at_top = (lax.broadcasted_iota(jnp.int32, (1, tile_rows), 1) == 0) & (
        lax.axis_index("row") == 0
    )
    charge_across = jnp.where(at_top, 0.0, charge_across)
    charge_down = (
        step_x[:, tile_rows - 1, 0:tile_cols]
        + step_y[:, tile_rows - 1, 1 : tile_cols + 1]
        - step_x[:, tile_rows, 0:tile_cols]
        - step_y[:, tile_rows - 1, 0:tile_cols]
    ) / TWO_PI
    at_left = (lax.broadcasted_iota(jnp.int32, (1, tile_cols), 1) == 0) & (
        lax.axis_index("col") == 0
    )
    charge_down = jnp.where(at_left, 0.0, charge_down)
    weight_across = 1.0 / (1.0 + jnp.abs(charge_across))
    weight_down = 1.0 / (1.0 + jnp.abs(charge_down))
    crossing_x = step_x[:, 1 : tile_rows + 1, tile_cols]
    crossing_y = step_y[:, tile_rows, 1 : tile_cols + 1]
    column_steps = step_y[:, 1 : tile_rows + 1, 1]
    downward = jnp.cumsum(column_steps, axis=1) - column_steps
    anchor = wrapped[:, 0, 0]
    integrated = (anchor[:, None] + downward)[:, :, None] + running_sum(
        step_x[:, 1 : tile_rows + 1, 1 : tile_cols + 1]
    )
    cycles_across = TWO_PI * col_steps[:, 0, 0].astype(jnp.float32)
    cycles_down = TWO_PI * row_steps[:, 0, 0].astype(jnp.float32)
    right_first = integrate_line(padded[:, 1 : tile_rows + 1, tile_cols + 1])
    below_first = integrate_line(padded[:, tile_rows + 1, 1 : tile_cols + 1])
    base_across = (
        mean_jump(integrated[:, :, -1], crossing_x, right_first, weight_across) + cycles_across
    )
    base_down = mean_jump(integrated[:, -1, :], crossing_y, below_first, weight_down) + cycles_down
    grid_rows = lax.axis_size("row")
    grid_cols = lax.axis_size("col")
    every_across, every_down = (
        lax.all_gather(base_across[:, None], ("row", "col"), axis=1, tiled=True),
        lax.all_gather(base_down[:, None], ("row", "col"), axis=1, tiled=True),
    )
    every_across = every_across.reshape(frames, grid_rows, grid_cols)
    every_down = every_down.reshape(frames, grid_rows, grid_cols)
    totals = jnp.zeros((frames, grid_rows, grid_cols), jnp.float32)
    for sweep in range(ITERS):
        right_total = jnp.concatenate(
            [totals[:, :, 1:], jnp.zeros((frames, grid_rows, 1), jnp.float32)], axis=2
        )
        below_total = jnp.concatenate(
            [totals[:, 1:, :], jnp.zeros((frames, 1, grid_cols), jnp.float32)], axis=1
        )
        horizontal = every_across + totals - right_total
        vertical = every_down + totals - below_total
        prefix_across = jnp.cumsum(horizontal, axis=2) - horizontal
        prefix_down = jnp.cumsum(vertical, axis=1) - vertical
        totals = totals + 0.5 * (
            prefix_across + prefix_across[:, 0:1, :] + prefix_down + prefix_down[:, :, 0:1]
        )
    mine = lax.dynamic_slice(
        totals, (0, lax.axis_index("row"), lax.axis_index("col")), (frames, 1, 1)
    )
    return (integrated + mine) / TWO_PI


def solution(mesh):
    in_specs = (P(None, "row", "col"), P(None, "row", "col"), P(None, "row", "col"))
    out_specs = P(None, "row", "col")
    return jax.shard_map(
        on_device, mesh=mesh, in_specs=in_specs, out_specs=out_specs, check_vma=False
    )
```

profile of v0, /device:TPU:0, one launch (start us, length us, event | category | flops | bytes accessed | tf_op | source)
XLA Modules:
  0.0 150.8 jit_solution(4451622152689461909)
XLA Ops:
  0.0 0.8 fusion.20
  0.8 0.2 copy.12
  1.0 1.3 collective-permute-start.1
  2.3 0.2 copy.11
  2.5 5.5 %collective-permute-start = (f32[1,1,1024]{1,2,0:T(8,128)S(1)}, f32[1,1,1024]{1,2,0:T(8,128)S(1)}, u32[]{:S(2)}, u32[]{:S(2)}) collective-permute-start(f32[1,1,1024]{1,2,0:T(8,128)S(1)} %copy.11), channel_id=1, source_target_pairs={{0,8},{8,16},{16,24},{1,9},{9,17},{17,25},{2,10},{10,18},{18,26},{... | collective-permute-start | bytes 12296 | tf_op jit(solution)/shard_map/ppermute | solution.py:22
  8.1 1.3 slice.126
  9.4 5.3 %copy.13 = f32[1,1024,1024]{1,2,0:T(8,128)} copy(f32[1,1024,1024]{2,1,0:T(8,128)} %param.3) | data formatting | bytes 8388608 | tf_op args[0]
  16.0 2.6 %collective-permute-done.1 = f32[1,1,1024]{1,2,0:T(8,128)S(1)} collective-permute-done((f32[1,1,1024]{1,2,0:T(8,128)S(1)}, f32[1,1,1024]{1,2,0:T(8,128)S(1)}, u32[]{:S(2)}, u32[]{:S(2)}) %collective-permute-start.1) | collective-permute-done | bytes 4128 | tf_op jit(solution)/shard_map/ppermute | solution.py:24
  18.7 0.2 reduce.10
  18.9 0.1 multiply_subtract_fusion.2
  19.0 0.3 reduce-window.26
  19.2 0.2 slice_reduce_fusion
  19.4 0.2 reduce-window.29
  19.6 0.0 collective-permute-done
  19.6 6.5 %concatenate.56 = f32[1,1026,1024]{1,2,0:T(8,128)} concatenate(f32[1,1,1024]{1,2,0:T(8,128)S(1)} %collective-permute-done, f32[1,1024,1024]{1,2,0:T(8,128)} %copy.13, f32[1,1,1024]{1,2,0:T(8,128)S(1)} %collective-permute-done.1), dimensions={1} | concatenate | bytes 8404992 | tf_op jit(solution)/shard_map/concatenate | solution.py:20
  26.1 0.8 fusion.19
  26.9 1.3 collective-permute-start.3
  28.2 0.1 broadcast.435
  28.3 0.6 slice.188
  28.8 3.0 %collective-permute-start.2 = (f32[1,1026,1]{1,2,0:T(1,128)S(1)}, f32[1,1026,1]{1,2,0:T(1,128)S(1)}, u32[]{:S(2)}, u32[]{:S(2)}) collective-permute-start(f32[1,1026,1]{1,2,0:T(1,128)S(1)} %get-tuple-element.14), channel_id=1, source_target_pairs={{0,1},{1,2},{2,3},{3,4},{4,5},{5,6},{6,7},{8,9},{9,10},{10,11},{11... | collective-permute-start | bytes 12320 | tf_op jit(solution)/shard_map/ppermute | solution.py:22
  31.9 0.0 collective-permute-done.3
  31.9 0.1 slice_bitcast_fusion
  32.0 0.1 multiply_subtract_fusion.3
  32.1 0.3 reduce-window.24
  32.4 0.2 slice_reduce_fusion.1
  32.5 0.2 reduce-window.25
  32.7 0.5 slice.179
  33.2 0.0 collective-permute-done.2
  33.2 15.3 %concatenate.57 = f32[1,1026,1026]{1,2,0:T(8,128)} concatenate(f32[1,1026,1]{1,2,0:T(1,128)S(1)} %collective-permute-done.2, f32[1,1026,1024]{1,2,0:T(8,128)} %concatenate.56, f32[1,1026,1]{1,2,0:T(1,128)S(1)} %collective-permute-done.3), dimensions={2} | concatenate | bytes 8421408 | tf_op jit(solution)/shard_map/concatenate | solution.py:20
  48.6 5.1 %multiply_subtract_fusion.1 = f32[1,1025,1026]{1,2,0:T(8,128)S(1)} fusion(f32[1,1026,1026]{1,2,0:T(8,128)} %concatenate.57), kind=kLoop, calls=%fused_computation.3 | loop fusion | flops 6309900 | bytes 12619800 | tf_op jit(solution)/shard_map/sub | solution.py:32
  53.7 0.0 copy-start.2
  53.7 2.1 %copy-done.2 = f32[1,1025,1026]{1,2,0:T(8,128)} copy-done((f32[1,1025,1026]{1,2,0:T(8,128)}, f32[1,1025,1026]{1,2,0:T(8,128)S(1)}, u32[]{:S(2)}) %copy-start.2) | copy-done | bytes 4206624
  55.8 0.1 slice.170
  55.9 0.3 reduce-window.20
  56.1 0.2 slice_reduce_fusion.2
  56.3 0.2 reduce-window.21
  56.5 5.9 %multiply_subtract_fusion = f32[1,1026,1025]{1,2,0:T(8,128)S(1)} fusion(f32[1,1026,1024]{1,2,0:T(8,128)} %concatenate.56, f32[1,1026,1]{1,2,0:T(1,128)S(1)} %collective-permute-done.2, f32[1,1026,1]{1,2,0:T(1,128)S(1)} %collective-permute-done.3), kind=kLoop, calls=%fused_computation.2 | loop fusion | flops 8413200 | bytes 8417304 | tf_op jit(solution)/shard_map/sub | solution.py:32
  62.5 0.0 copy-start.1
  62.5 2.2 %copy-done.1 = f32[1,1026,1025]{1,2,0:T(8,128)} copy-done((f32[1,1026,1025]{1,2,0:T(8,128)}, f32[1,1026,1025]{1,2,0:T(8,128)S(1)}, u32[]{:S(2)}) %copy-start.1) | copy-done | bytes 4206624
  64.6 3.4 %slice.171 = f32[1,1024,1024]{1,2,0:T(8,128)} slice(f32[1,1026,1025]{1,2,0:T(8,128)S(1)} %multiply_subtract_fusion), slice={[0:1], [1:1025], [1:1025]} | slice | bytes 8388608 | tf_op jit(solution)/shard_map/slice | solution.py:93
  68.0 2.6 %reduce_sum.45 = f32[1024,8]{0,1:T(8,128)S(1)} reduce(f32[1024,8,128]{0,2,1:T(8,128)} %bitcast.61, f32[]{:T(128)} %constant.55.clone.1), dimensions={2}, to_apply=%region_2.3 | reduce | flops 1040384 | bytes 4227076 | tf_op jit(solution)/shard_map/reduce_sum | solution.py:45
  70.7 5.3 %convolution_add_fusion = f32[1024,8,128]{0,2,1:T(8,128)S(1)} fusion(f32[1024,8,128]{0,2,1:T(8,128)} %bitcast.62, f32[1024,8]{0,1:T(8,128)S(1)} %sub.200), kind=kOutput, calls=%fused_computation.6 | convolution fusion | flops 1611677696 | bytes 8421376 | tf_op jit(solution)/shard_map/frcm,mk->frck/dot_general | solution.py:44
  76.0 0.0 copy-start
  76.0 0.1 broadcast.424
  76.1 1.6 %subtract_add_fusion = f32[1,1024,1]{1,2,0:T(1,128)S(1)} fusion(f32[1,1024,1]{1,2,0:T(1,128)S(1)} %bitcast.69, f32[1,1024,1]{1,2,0:T(1,128)S(1)} %bitcast.77, f32[]{:T(128)} %bitcast, f32[1,1025,1026]{1,2,0:T(8,128)} %copy-done.2), kind=kLoop, calls=%fused_computation.43 | loop fusion | flops 3072 | bytes 16388 | tf_op jit(solution)/shard_map/add | solution.py:92
  77.7 0.8 bitcast_add_fusion
  78.5 2.6 %fusion = (f32[1024]{0:T(1024)S(1)}, f32[1024]{0:T(1024)S(1)}) fusion(f32[1,1025,1026]{1,2,0:T(8,128)} %copy-done.2, f32[1,1024,1024]{1,2,0:T(8,128)S(1)} %bitcast_add_fusion, f32[1,1026,1025]{1,2,0:T(8,128)} %copy-done.1), kind=kLoop, calls=%fused_computation.8 | loop fusion | flops 5120 | bytes 32768 | tf_op jit(solution)/shard_map/add | solution.py:57
  81.1 0.1 broadcast.433
  81.2 2.9 %fusion.17 = (f32[]{:T(128)}, f32[]{:T(128)}, f32[]{:T(128)}, f32[]{:T(128)}) fusion(f32[1,1023]{1,0:T(1,128)S(1)} %slice_add_fusion.3, f32[1,1]{1,0:T(1,128)} %constant.59.clone.1, f32[]{:T(128)} %bitcast.12, f32[1,1026,1025]{1,2,0:T(8,128)} %copy-done.1, f32[1,1024,1024]{1,2,0:T(8,128)S(1)} %bitcast_add_fusion, f32[1,1025,1026]{1,2,0:T(8,128)} %copy-done.2, ...), kind=kLoop, calls=%fused_computation.63 | loop fusion | flops 28668 | bytes 40982 | tf_op jit(solution)/shard_map/reduce_sum | solution.py:57
  86.7 0.1 fusion.16
  86.8 0.1 fusion.15
  86.9 51.2 %all-reduce.6 = (f32[32]{0:T(128)S(1)}, f32[32]{0:T(128)S(1)}) all-reduce(f32[32]{0:T(128)S(1)} %fusion.15, f32[32]{0:T(128)S(1)} %fusion.16), channel_id=3, replica_groups=mesh['row'=4,'col'=8] {'row','col'}, use_global_device_ids=true, to_apply=%add.5 | all-reduce | flops 64 | bytes 512
  138.1 0.1 reshape.901
  138.2 0.1 slice_reduce_fusion.4
  138.3 0.1 reshape.895
  138.4 0.2 reduce_window_sum.105
  138.6 0.1 add_multiply_fusion.1
  138.7 0.1 slice.162
  138.8 0.2 reduce_window_sum.108
  139.0 0.1 slice_reduce_fusion.3
  139.1 0.1 multiply_add_fusion
  139.2 0.6 constant_dynamic-slice_fusion
  139.8 5.7 %add_multiply_fusion = f32[1,1024,1024]{1,2,0:T(8,128)} fusion(f32[]{:T(128)} %bitcast.28, f32[1024,8,128]{0,2,1:T(8,128)} %copy-done, f32[1024]{0:T(1024)S(1)} %bitcast.64), kind=kLoop, calls=%fused_computation.5 | loop fusion | flops 3145728 | bytes 8392708 | tf_op jit(solution)/shard_map/div | solution.py:129
  145.5 5.3 %copy.15 = f32[1,1024,1024]{2,1,0:T(8,128)} copy(f32[1,1024,1024]{1,2,0:T(8,128)} %add_multiply_fusion) | data formatting | bytes 8388608 | tf_op jit(solution)/shard_map/div | solution.py:129
  (22 shorter events, 0.2 us)
Async XLA Ops:
  1.0 17.6 %collective-permute-start.1 = (f32[1,1,1024]{1,2,0:T(8,128)S(1)}, f32[1,1,1024]{1,2,0:T(8,128)S(1)}, u32[]{:S(2)}, u32[]{:S(2)}) collective-permute-start(f32[1,1,1024]{1,2,0:T(8,128)S(1)} %copy.12), channel_id=1, source_target_pairs={{8,0},{16,8},{24,16},{9,1},{17,9},{25,17},{10,2},{18,10},{26,18},{... | collective-permute-start | bytes 12296 | tf_op jit(solution)/shard_map/ppermute | solution.py:24
  2.5 17.1 %collective-permute-start = (f32[1,1,1024]{1,2,0:T(8,128)S(1)}, f32[1,1,1024]{1,2,0:T(8,128)S(1)}, u32[]{:S(2)}, u32[]{:S(2)}) collective-permute-start(f32[1,1,1024]{1,2,0:T(8,128)S(1)} %copy.11), channel_id=1, source_target_pairs={{0,8},{8,16},{16,24},{1,9},{9,17},{17,25},{2,10},{10,18},{18,26},{... | collective-permute-start | bytes 12296 | tf_op jit(solution)/shard_map/ppermute | solution.py:22
  26.9 5.0 %collective-permute-start.3 = (f32[1,1026,1]{1,2,0:T(1,128)S(1)}, f32[1,1026,1]{1,2,0:T(1,128)S(1)}, u32[]{:S(2)}, u32[]{:S(2)}) collective-permute-start(f32[1,1026,1]{1,2,0:T(1,128)S(1)} %get-tuple-element.13), channel_id=1, source_target_pairs={{1,0},{2,1},{3,2},{4,3},{5,4},{6,5},{7,6},{9,8},{10,9},{11,10},{12... | collective-permute-start | bytes 12320 | tf_op jit(solution)/shard_map/ppermute | solution.py:24
  28.8 4.4 %collective-permute-start.2 = (f32[1,1026,1]{1,2,0:T(1,128)S(1)}, f32[1,1026,1]{1,2,0:T(1,128)S(1)}, u32[]{:S(2)}, u32[]{:S(2)}) collective-permute-start(f32[1,1026,1]{1,2,0:T(1,128)S(1)} %get-tuple-element.14), channel_id=1, source_target_pairs={{0,1},{1,2},{2,3},{3,4},{4,5},{5,6},{6,7},{8,9},{9,10},{10,11},{11... | collective-permute-start | bytes 12320 | tf_op jit(solution)/shard_map/ppermute | solution.py:22
  53.7 2.1 %copy-start.2 = (f32[1,1025,1026]{1,2,0:T(8,128)}, f32[1,1025,1026]{1,2,0:T(8,128)S(1)}, u32[]{:S(2)}) copy-start(f32[1,1025,1026]{1,2,0:T(8,128)S(1)} %multiply_subtract_fusion.1) | copy-start | bytes 12619804
  62.5 2.2 %copy-start.1 = (f32[1,1026,1025]{1,2,0:T(8,128)}, f32[1,1026,1025]{1,2,0:T(8,128)S(1)}, u32[]{:S(2)}) copy-start(f32[1,1026,1025]{1,2,0:T(8,128)S(1)} %multiply_subtract_fusion) | copy-start | bytes 12619804
  76.0 5.1 %copy-start = (f32[1024,8,128]{0,2,1:T(8,128)}, f32[1024,8,128]{0,2,1:T(8,128)S(1)}, u32[]{:S(2)}) copy-start(f32[1024,8,128]{0,2,1:T(8,128)S(1)} %convolution_add_fusion) | copy-start | bytes 12582916
where the time goes:
time: 152 us; the launch traced here: 151 us
  blocking collectives  51.2 us (34%)
  local copies, waits for them, and re-layouts  46.6 us (31%)
  other arithmetic  29.9 us (20%)
  starting transfers between devices  11.1 us (7%)
  matrix products  5.29 us (3%)
  between operations  4.11 us (3%)
  waiting for transfers between devices  2.64 us (2%)
    unnamed x1, blocking collectives  51.2 us
    concatenate x2, local copies, waits for them, and re-layouts, extended(): jnp.concatenate([lax.ppermute(tail, axis, [(i, (i + 1) % count) for i in...  21.8 us
    sub x4, other arithmetic, wrap_diff(): return change - TWO_PI * jnp.floor(change / TWO_PI + 0.5)  11.2 us
    unnamed x9, local copies, waits for them, and re-layouts  9.64 us
    ppermute x2, starting transfers between devices, extended(): lax.ppermute(tail, axis, [(i, (i + 1) % count) for i in range(ends)])  8.55 us
    div x1, other arithmetic, on_device(): return (integrated + mine) / TWO_PI  5.7 us
    div x1, local copies, waits for them, and re-layouts, on_device(): return (integrated + mine) / TWO_PI  5.34 us
    dot_general x1, matrix products, running_sum(): jnp.einsum('frcm,mk->frck', pieces, strict_upper, precision=lax.Precision...  5.29 us
  transfers between devices with their start and end apart: 4, of which 1 were waited for; matrix products, arithmetic and copies ran while one was open for 6% of the time, Pallas kernels for 0%

commit v1 on v0

v1 whole, which is shorter than its diff:
```python
import functools
import math

import jax
import jax.numpy as jnp
from jax import lax
from jax.experimental import pallas as pl
from jax.experimental.pallas import tpu as pltpu
from jax.sharding import PartitionSpec as P

ITERS = 2
TWO_PI = 2.0 * math.pi
CYCLE = 1.0 / TWO_PI
LANES = 128


def iota(shape, dim):
    return lax.broadcasted_iota(jnp.int32, shape, dim)


def wraps(change):
    return jnp.floor(change + 0.5)


def along(line):
    return jnp.where(iota(line.shape, 1) == 0, 0.0, wraps(line - pltpu.roll(line, 1, 1)))


def upper_ones(length, width):
    shape = (length, width)
    return (iota(shape, 0) - (length - width) <= iota(shape, 1)).astype(jnp.bfloat16)


def prefix_blocks(counts, ones, width):
    length = counts.shape[1]
    narrow = counts.astype(jnp.bfloat16)
    return [
        jnp.dot(narrow[:, :stop], ones[length - stop :, :], preferred_element_type=jnp.float32)
        for stop in range(width, length + 1, width)
    ]


def integrate_kernel(w_ref, u_ref, cols_ref, rows_ref, ones, lower, last_phase, last_wraps, *, width):
    height, length = w_ref.shape
    step = pl.program_id(0)
    phase = w_ref[...] * CYCLE
    edge = phase[:, :LANES]

    @pl.when(step == 0)
    def _():
        ones[...] = upper_ones(length, width)
        lower[...] = (iota((height, height), 0) >= iota((height, height), 1)).astype(jnp.bfloat16)
        last_phase[...] = edge[0:1, :]
        last_wraps[...] = jnp.zeros_like(last_wraps)

    before = jnp.where(iota(edge.shape, 0) == 0, last_phase[...], pltpu.roll(edge, 1, 0))
    down = wraps(edge - before).astype(jnp.bfloat16)
    down = jnp.dot(lower[...], down, preferred_element_type=jnp.float32) + last_wraps[...]
    last_phase[...] = edge[height - 1 :, :]
    last_wraps[...] = down[height - 1 :, :]
    first = down[:, 0:1]
    blocks = prefix_blocks(along(phase), ones, width)
    for n, block in enumerate(blocks):
        span = slice(n * width, (n + 1) * width)
        total = first + block
        u_ref[:, span] = phase[:, span] - total
        rows_ref[0:1, span] = total[height - 1 :, :]
    rows_ref[1:3, :] = phase[height - 2 :, :]
    cols_ref[0:1, :] = total[:, width - LANES :].T[LANES - 1 :, :]
    cols_ref[1:3, :] = phase[:, length - LANES :].T[LANES - 2 :, :]


def side_sums(lines, halo, at_end, width):
    total, inner, outer = lines[0:1, :], lines[1:2, :], lines[2:3, :]
    lane = iota(total.shape, 1)
    length = total.shape[1]
    outer_wraps, halo_wraps = along(outer), along(halo)
    cross = wraps(outer - inner)
    charge = along(inner) + cross - outer_wraps - pltpu.roll(cross, 1, 1)
    weight = jnp.where(lane == 0, 0.0, 1.0 / (1.0 + jnp.abs(charge)))
    beyond = wraps(halo - outer)
    next_charge = outer_wraps + beyond - halo_wraps - pltpu.roll(beyond, 1, 1)
    next_weight = 1.0 / (1.0 + jnp.abs(next_charge))
    ones = upper_ones(length, width)
    halo_total = jnp.concatenate(
        [b[0:1, :] for b in prefix_blocks(jnp.broadcast_to(halo_wraps, (8, length)), ones, width)],
        axis=1,
    )
    jump = jnp.where(at_end, outer - total, halo_total - total - beyond)

    def add(values):
        return jnp.sum(values, axis=1, keepdims=True)

    return [
        add(weight * jump),
        add(weight),
        add(jnp.where(lane == 0, jump, 0.0)),
        add(jnp.where(lane == length - 1, next_weight, 0.0)),
    ]


def edges_kernel(
    right_steps, down_steps, cols_ref, rows_ref, right_ref, below_ref, table_ref, *, grid, widths
):
    row, col = lax.axis_index("row"), lax.axis_index("col")
    values = side_sums(cols_ref[...], right_ref[...] * CYCLE, col == grid[1] - 1, widths[0])
    values += side_sums(rows_ref[...], below_ref[...] * CYCLE, row == grid[0] - 1, widths[1])
    shape = table_ref.shape
    values += [
        jnp.full((1, 1), right_steps[0].astype(jnp.float32)),
        jnp.full((1, 1), down_steps[0].astype(jnp.float32)),
    ]
    table = jnp.zeros(shape, jnp.float32)
    for n, value in enumerate(values):
        table = jnp.where(iota(shape, 0) == n, value, table)
    table_ref[...] = jnp.where(iota(shape, 1) == row * grid[1] + col, table, 0.0)


def tile_offsets(table, grid):
    tile_rows, tile_cols = grid
    shape = (8, table.shape[1])
    size = table.shape[1]
    lane = iota(shape, 1)
    r, c = lane // tile_cols, lane % tile_cols
    there = lane < tile_rows * tile_cols

    def line(n):
        return jnp.broadcast_to(table[n : n + 1, :], shape)

    first = jnp.where(r == 0, 1.0, pltpu.roll(line(7), tile_cols, 1))
    across = (line(0) + first * line(2)) / (line(1) + first) + line(8)
    across = jnp.where(there, across, 0.0)
    first = jnp.where(c == 0, 1.0, pltpu.roll(line(3), 1, 1))
    down = (line(4) + first * line(6)) / (line(5) + first) + line(9)
    down = jnp.where(there, down, 0.0)
    source, target = iota((size, size), 0), iota((size, size), 1)
    sr, sc = source // tile_cols, source % tile_cols
    tr, tc = target // tile_cols, target % tile_cols
    use_across = jnp.where(sc < tc, 0.5, 0.0)
    use_across = jnp.where(sr == tr, use_across, 0.0) + jnp.where(sr == 0, use_across, 0.0)
    use_down = jnp.where(sr < tr, 0.5, 0.0)
    use_down = jnp.where(sc == tc, use_down, 0.0) + jnp.where(sc == 0, use_down, 0.0)
    dot = functools.partial(
        jnp.dot, precision=lax.Precision.HIGHEST, preferred_element_type=jnp.float32
    )
    totals = jnp.zeros(shape, jnp.float32)
    for _ in range(ITERS):
        right = jnp.where(c == tile_cols - 1, 0.0, pltpu.roll(totals, size - 1, 1))
        below = jnp.where(r == tile_rows - 1, 0.0, pltpu.roll(totals, size - tile_cols, 1))
        horizontal = across + totals - right
        vertical = down + totals - below
        step = dot(horizontal, use_across) + dot(vertical, use_down)
        totals = totals + jnp.where(there, step, 0.0)
    return totals


def shift_kernel(table_ref, u_ref, out_ref, offset, *, grid):
    @pl.when(pl.program_id(0) == 0)
    def _():
        totals = tile_offsets(table_ref[...], grid)[0:1, :]
        me = lax.axis_index("row") * grid[1] + lax.axis_index("col")
        mine = jnp.sum(jnp.where(iota(totals.shape, 1) == me, totals, 0.0), axis=1, keepdims=True)
        offset[...] = jnp.broadcast_to(mine, offset.shape)

    out_ref[...] = u_ref[...] + offset[0:1, 0:1]


def integrate(tile):
    rows, cols = tile.shape
    height, width = math.gcd(rows, 256), math.gcd(cols, 256)
    return pl.pallas_call(
        functools.partial(integrate_kernel, width=width),
        grid=(rows // height,),
        in_specs=[pl.BlockSpec((height, cols), lambda i: (i, 0))],
        out_specs=[
            pl.BlockSpec((height, cols), lambda i: (i, 0)),
            pl.BlockSpec((8, height), lambda i: (0, i)),
            pl.BlockSpec((8, cols), lambda i: (0, 0)),
        ],
        out_shape=[
            jax.ShapeDtypeStruct((rows, cols), jnp.float32),
            jax.ShapeDtypeStruct((8, rows), jnp.float32),
            jax.ShapeDtypeStruct((8, cols), jnp.float32),
        ],
        scratch_shapes=[
            pltpu.VMEM((cols, width), jnp.bfloat16),
            pltpu.VMEM((height, height), jnp.bfloat16),
            pltpu.VMEM((1, LANES), jnp.float32),
            pltpu.VMEM((1, LANES), jnp.float32),
        ],
        name="integrate",
    )(tile)


def gathered(table, grid):
    for axis, count in zip(("col", "row"), grid[::-1]):
        if count & (count - 1):
            table = lax.psum(table, axis)
            continue
        bit = 1
        while bit < count:
            table = table + lax.ppermute(table, axis, [(i, i ^ bit) for i in range(count)])
            bit *= 2
    return table


def on_device(grid, wrapped, col_steps, row_steps):
    frames, rows, cols = wrapped.shape
    widths = (math.gcd(rows, 256), math.gcd(cols, 256))
    slots = -(-grid[0] * grid[1] // LANES) * LANES
    smem = pl.BlockSpec(memory_space=pltpu.SMEM)
    vmem = pl.BlockSpec(memory_space=pltpu.VMEM)
    outs = []
    for f in range(frames):
        tile = wrapped[f]
        right = lax.ppermute(tile[:, 0][None, :], "col", [(i + 1, i) for i in range(grid[1] - 1)])
        below = lax.ppermute(tile[0:1, :], "row", [(i + 1, i) for i in range(grid[0] - 1)])
        cycles, col_lines, row_lines = integrate(tile)
        table = pl.pallas_call(
            functools.partial(edges_kernel, grid=grid, widths=widths),
            in_specs=[smem, smem, vmem, vmem, vmem, vmem],
            out_specs=vmem,
            out_shape=jax.ShapeDtypeStruct((16, slots), jnp.float32),
            name="edges",
        )(col_steps[f, 0], row_steps[f, 0], col_lines, row_lines, right, below)
        table = gathered(table, grid)
        height = math.gcd(rows, 256)
        outs.append(
            pl.pallas_call(
                functools.partial(shift_kernel, grid=grid),
                grid=(rows // height,),
                in_specs=[
                    pl.BlockSpec((16, slots), lambda i: (0, 0)),
                    pl.BlockSpec((height, cols), lambda i: (i, 0)),
                ],
                out_specs=pl.BlockSpec((height, cols), lambda i: (i, 0)),
                out_shape=jax.ShapeDtypeStruct((rows, cols), jnp.float32),
                scratch_shapes=[pltpu.VMEM((8, LANES), jnp.float32)],
                name="shift",
            )(table, cycles)
        )
    return jnp.stack(outs)


def solution(mesh):
    grid = (mesh.shape["row"], mesh.shape["col"])
    spec = P(None, "row", "col")
    return jax.shard_map(
        functools.partial(on_device, grid),
        mesh=mesh,
        in_specs=(spec, spec, spec),
        out_specs=spec,
        check_vma=False,
    )
```

time: 152 us -> 43.1 us (0.28)
  blocking collectives: 51.2 us -> 0 us
  local copies, waits for them, and re-layouts: 46.6 us -> 2.59 us
  other arithmetic: 29.9 us -> 1.3 us
  Pallas kernels: 0 us -> 14.1 us
  matrix products: 5.29 us -> 0 us
  waiting for transfers between devices: 2.64 us -> 7.56 us
  starting transfers between devices: 11.1 us -> 15.7 us
  between operations: 4.11 us -> 1.36 us
    unnamed x1 -> x0, blocking collectives: 51.2 us -> none
    concatenate x2 -> x0, local copies, waits for them, and re-layouts: 21.8 us -> none  [extended(): jnp.concatenate([lax.ppermute(tail, axis, [(i, (i + 1) % count) for i in...]
    pallas_call x0 -> x3, Pallas kernels: none -> 14.1 us  [the longest x1 6.48 us: integrate(): pl.pallas_call(functools.partial(integrate_kernel, width=width), grid=(ro...]
    sub x10 -> x0, other arithmetic: 11.2 us -> none  [the longest x4 11.2 us: wrap_diff(): return change - TWO_PI * jnp.floor(change / TWO_PI + 0.5)]
    unnamed x9 -> x4, local copies, waits for them, and re-layouts: 9.64 us -> 0.58 us
    slice x14 -> x2, local copies, waits for them, and re-layouts: 8.37 us -> 2.01 us  [the longest x1 1.25 us: on_device(): tile[:, 0][None, :]]
    div x1 -> x0, other arithmetic: 5.7 us -> none  [on_device(): return (integrated + mine) / TWO_PI]
    reduce_sum x2 -> x0, other arithmetic: 5.48 us -> none  [the longest x1 2.87 us: mean_jump(): jnp.sum(weights, axis=1)]
  transfers between devices with their start and end apart: 4 -> 7, of which waited for: 1 -> 5; matrix products, arithmetic and copies ran while one was open for 6% -> 3% of each run, Pallas kernels for 0% -> 15%
where the time goes in v1:
time: 43.1 us; the launch traced here: 42.6 us
  starting transfers between devices  15.7 us (36%)
  Pallas kernels  14.1 us (33%)
  waiting for transfers between devices  7.56 us (18%)
  local copies, waits for them, and re-layouts  2.59 us (6%)
  between operations  1.36 us (3%)
  other arithmetic  1.3 us (3%)
    ppermute x5, starting transfers between devices, gathered(): lax.ppermute(table, axis, [(i, i ^ bit) for i in range(count)])  13.1 us
    ppermute x5, waiting for transfers between devices, gathered(): lax.ppermute(table, axis, [(i, i ^ bit) for i in range(count)])  7.55 us
    pallas_call x1, Pallas kernels, integrate(): pl.pallas_call(functools.partial(integrate_kernel, width=width), grid=(ro...  6.48 us
    pallas_call x1, Pallas kernels, on_device(): pl.pallas_call(functools.partial(shift_kernel, grid=grid), grid=(rows //...  5.61 us
    pallas_call x1, Pallas kernels, on_device(): pl.pallas_call(functools.partial(edges_kernel, grid=grid, widths=widths),...  1.97 us
    add x5, other arithmetic, gathered(): table + lax.ppermute(table, axis, [(i, i ^ bit) for i in range(count)])  1.3 us
    ppermute x1, starting transfers between devices, on_device(): lax.ppermute(tile[:, 0][None, :], 'col', [(i + 1, i) for i in range(grid[...  1.29 us
    ppermute x1, starting transfers between devices, on_device(): lax.ppermute(tile[0:1, :], 'row', [(i + 1, i) for i in range(grid[0] - 1)])  1.28 us
  transfers between devices with their start and end apart: 7, of which 5 were waited for; matrix products, arithmetic and copies ran while one was open for 3% of the time, Pallas kernels for 15%

profile of v1, /device:TPU:0, one launch (start us, length us, event | category | flops | bytes accessed | tf_op | source)
XLA Modules:
  0.0 42.6 jit_solution(11534759531632437118)
XLA Ops:
  0.0 0.8 %slice_bitcast_fusion = f32[1,1024]{1,0:T(1,128)S(1)} fusion(f32[1,1024,1024]{2,1,0:T(8,128)} %param.3), kind=kLoop, calls=%fused_computation.1 | loop fusion | bytes 8192 | tf_op jit(solution)/shard_map/slice | solution.py:217
  0.8 1.3 %collective-permute-start.1 = (f32[1,1024]{1,0:T(1,128)S(1)}, f32[1,1024]{1,0:T(1,128)S(1)}, u32[]{:S(2)}, u32[]{:S(2)}) collective-permute-start(f32[1,1024]{1,0:T(1,128)S(1)} %slice_bitcast_fusion), channel_id=1, source_target_pairs={{8,0},{16,8},{24,16},{9,1},{17,9},{25,17},{10,2},{18,10},{26,18},{... | collective-permute-start | bytes 12296 | tf_op jit(solution)/shard_map/ppermute | solution.py:217
  2.0 1.2 %slice_reduce_fusion = f32[1024]{0:T(1024)S(1)} fusion(f32[1024,1024]{1,0:T(8,128)} %bitcast.9), kind=kLoop, calls=%fused_computation | loop fusion | bytes 8192 | tf_op jit(solution)/shard_map/slice | solution.py:216
  3.3 1.3 %collective-permute-start = (f32[1,1024]{1,0:T(1,128)S(1)}, f32[1,1024]{1,0:T(1,128)S(1)}, u32[]{:S(2)}, u32[]{:S(2)}) collective-permute-start(f32[1,1024]{1,0:T(1,128)S(1)} %bitcast.11), channel_id=1, source_target_pairs={{1,0},{2,1},{3,2},{4,3},{5,4},{6,5},{7,6},{9,8},{10,9},{11,10},{12... | collective-permute-start | bytes 12296 | tf_op jit(solution)/shard_map/ppermute | solution.py:216
  4.6 6.5 %integrate.1 = (f32[1024,1024]{1,0:T(8,128)}, f32[8,1024]{1,0:T(8,128)}, f32[8,1024]{1,0:T(8,128)}) custom-call(f32[1024,1024]{1,0:T(8,128)} %bitcast.10), custom_call_target="tpu_custom_call" | custom-call | tf_op jit(solution)/shard_map/integrate/pallas_call | solution.py:171
  12.4 0.0 collective-permute-done.1.below_ref
  12.4 0.0 copy-start
  12.4 0.0 collective-permute-done.right_ref
  12.4 0.0 copy-start.1
  12.4 0.6 %copy-done = f32[1,1024]{1,0:T(1,128)} copy-done((f32[1,1024]{1,0:T(1,128)}, f32[1,1024]{1,0:T(1,128)S(1)}, u32[]{:S(2)}) %copy-start) | copy-done | bytes 4120
  13.0 0.0 copy-done.1
  13.0 2.0 %edges.1 = f32[16,128]{1,0:T(8,128)} custom-call(s32[1]{0:T(128)} %bitcast.7.right_steps, s32[1]{0:T(128)} %bitcast.8.down_steps, f32[8,1024]{1,0:T(8,128)} %get-tuple-element.8.cols_ref, f32[8,1024]{1,0:T(8,128)} %get-tuple-element.9.rows_ref, f32[1,1024]{1,0:T(1,128)} %copy-done.1, f32[1,1024]{1,0:T(1,128)} %copy-done), custom_call_target="tpu_custom_call" | custom-call | tf_op jit(solution)/shard_map/edges/pallas_call | solution.py:219
  15.0 1.1 %collective-permute-start.2 = (f32[16,128]{1,0:T(8,128)}, f32[16,128]{1,0:T(8,128)S(1)}, u32[]{:S(2)}, u32[]{:S(2)}) collective-permute-start(f32[16,128]{1,0:T(8,128)} %edges.1), channel_id=1, source_target_pairs={{0,1},{1,0},{2,3},{3,2},{4,5},{5,4},{6,7},{7,6},{8,9},{9,8},{10,11... | collective-permute-start | bytes 24584 | tf_op jit(solution)/shard_map/ppermute | solution.py:202
  16.1 1.0 %collective-permute-done.2 = f32[16,128]{1,0:T(8,128)S(1)} collective-permute-done((f32[16,128]{1,0:T(8,128)}, f32[16,128]{1,0:T(8,128)S(1)}, u32[]{:S(2)}, u32[]{:S(2)}) %collective-permute-start.2) | collective-permute-done | bytes 8224 | tf_op jit(solution)/shard_map/ppermute | solution.py:202
  17.1 0.7 %add.15 = f32[16,128]{1,0:T(8,128)S(1)} add(f32[16,128]{1,0:T(8,128)} %edges.1, f32[16,128]{1,0:T(8,128)S(1)} %collective-permute-done.2) | non-fusion elementwise | flops 2048 | bytes 24576 | tf_op jit(solution)/shard_map/add | solution.py:202
  17.8 3.1 %collective-permute-start.3 = (f32[16,128]{1,0:T(8,128)S(1)}, f32[16,128]{1,0:T(8,128)S(1)}, u32[]{:S(2)}, u32[]{:S(2)}) collective-permute-start(f32[16,128]{1,0:T(8,128)S(1)} %add.15), channel_id=1, source_target_pairs={{0,2},{1,3},{2,0},{3,1},{4,6},{5,7},{6,4},{7,5},{8,10},{9,11},{10,... | collective-permute-start | bytes 24584 | tf_op jit(solution)/shard_map/ppermute | solution.py:202
  20.9 1.6 %collective-permute-done.3 = f32[16,128]{1,0:T(8,128)S(1)} collective-permute-done((f32[16,128]{1,0:T(8,128)S(1)}, f32[16,128]{1,0:T(8,128)S(1)}, u32[]{:S(2)}, u32[]{:S(2)}) %collective-permute-start.3) | collective-permute-done | bytes 8224 | tf_op jit(solution)/shard_map/ppermute | solution.py:202
  22.5 3.0 %collective-permute-start.4 = (f32[16,128]{1,0:T(8,128)S(1)}, f32[16,128]{1,0:T(8,128)S(1)}, u32[]{:S(2)}, u32[]{:S(2)}) collective-permute-start(f32[16,128]{1,0:T(8,128)S(1)} %add.16), channel_id=1, source_target_pairs={{0,4},{1,5},{2,6},{3,7},{4,0},{5,1},{6,2},{7,3},{8,12},{9,13},{10,... | collective-permute-start | bytes 24584 | tf_op jit(solution)/shard_map/ppermute | solution.py:202
  25.6 1.6 %collective-permute-done.4 = f32[16,128]{1,0:T(8,128)S(1)} collective-permute-done((f32[16,128]{1,0:T(8,128)S(1)}, f32[16,128]{1,0:T(8,128)S(1)}, u32[]{:S(2)}, u32[]{:S(2)}) %collective-permute-start.4) | collective-permute-done | bytes 8224 | tf_op jit(solution)/shard_map/ppermute | solution.py:202
  27.2 2.6 %collective-permute-start.5 = (f32[16,128]{1,0:T(8,128)S(1)}, f32[16,128]{1,0:T(8,128)S(1)}, u32[]{:S(2)}, u32[]{:S(2)}) collective-permute-start(f32[16,128]{1,0:T(8,128)S(1)} %add.17), channel_id=1, source_target_pairs={{0,8},{8,0},{16,24},{24,16},{1,9},{9,1},{17,25},{25,17},{2,10},{10... | collective-permute-start | bytes 24584 | tf_op jit(solution)/shard_map/ppermute | solution.py:202
  29.8 1.6 %collective-permute-done.5 = f32[16,128]{1,0:T(8,128)S(1)} collective-permute-done((f32[16,128]{1,0:T(8,128)S(1)}, f32[16,128]{1,0:T(8,128)S(1)}, u32[]{:S(2)}, u32[]{:S(2)}) %collective-permute-start.5) | collective-permute-done | bytes 8224 | tf_op jit(solution)/shard_map/ppermute | solution.py:202
  31.5 3.3 %collective-permute-start.6 = (f32[16,128]{1,0:T(8,128)S(1)}, f32[16,128]{1,0:T(8,128)S(1)}, u32[]{:S(2)}, u32[]{:S(2)}) collective-permute-start(f32[16,128]{1,0:T(8,128)S(1)} %add.18), channel_id=1, source_target_pairs={{0,16},{8,24},{16,0},{24,8},{1,17},{9,25},{17,1},{25,9},{2,18},{10... | collective-permute-start | bytes 24584 | tf_op jit(solution)/shard_map/ppermute | solution.py:202
  34.7 1.6 %collective-permute-done.6 = f32[16,128]{1,0:T(8,128)S(1)} collective-permute-done((f32[16,128]{1,0:T(8,128)S(1)}, f32[16,128]{1,0:T(8,128)S(1)}, u32[]{:S(2)}, u32[]{:S(2)}) %collective-permute-start.6) | collective-permute-done | bytes 8224 | tf_op jit(solution)/shard_map/ppermute | solution.py:202
  36.4 0.6 %add.19.table_ref = f32[16,128]{1,0:T(8,128)} add(f32[16,128]{1,0:T(8,128)S(1)} %add.18, f32[16,128]{1,0:T(8,128)S(1)} %collective-permute-done.6) | non-fusion elementwise | flops 2048 | bytes 24576 | tf_op jit(solution)/shard_map/add | solution.py:202
  37.0 5.6 %shift.1 = f32[1024,1024]{1,0:T(8,128)} custom-call(f32[16,128]{1,0:T(8,128)} %add.19.table_ref, f32[1024,1024]{1,0:T(8,128)} %get-tuple-element.10.u_ref), custom_call_target="tpu_custom_call" | custom-call | tf_op jit(solution)/shard_map/shift/pallas_call | solution.py:229
  (3 shorter events, 0.0 us)
Async XLA Ops:
  0.8 11.6 %collective-permute-start.1 = (f32[1,1024]{1,0:T(1,128)S(1)}, f32[1,1024]{1,0:T(1,128)S(1)}, u32[]{:S(2)}, u32[]{:S(2)}) collective-permute-start(f32[1,1024]{1,0:T(1,128)S(1)} %slice_bitcast_fusion), channel_id=1, source_target_pairs={{8,0},{16,8},{24,16},{9,1},{17,9},{25,17},{10,2},{18,10},{26,18},{... | collective-permute-start | bytes 12296 | tf_op jit(solution)/shard_map/ppermute | solution.py:217
  3.3 9.1 %collective-permute-start = (f32[1,1024]{1,0:T(1,128)S(1)}, f32[1,1024]{1,0:T(1,128)S(1)}, u32[]{:S(2)}, u32[]{:S(2)}) collective-permute-start(f32[1,1024]{1,0:T(1,128)S(1)} %bitcast.11), channel_id=1, source_target_pairs={{1,0},{2,1},{3,2},{4,3},{5,4},{6,5},{7,6},{9,8},{10,9},{11,10},{12... | collective-permute-start | bytes 12296 | tf_op jit(solution)/shard_map/ppermute | solution.py:216
  12.4 0.6 %copy-start = (f32[1,1024]{1,0:T(1,128)}, f32[1,1024]{1,0:T(1,128)S(1)}, u32[]{:S(2)}) copy-start(f32[1,1024]{1,0:T(1,128)S(1)} %collective-permute-done.1.below_ref) | copy-start | bytes 12292
  12.4 0.6 %copy-start.1 = (f32[1,1024]{1,0:T(1,128)}, f32[1,1024]{1,0:T(1,128)S(1)}, u32[]{:S(2)}) copy-start(f32[1,1024]{1,0:T(1,128)S(1)} %collective-permute-done.right_ref) | copy-start | bytes 12292
  15.0 2.2 %collective-permute-start.2 = (f32[16,128]{1,0:T(8,128)}, f32[16,128]{1,0:T(8,128)S(1)}, u32[]{:S(2)}, u32[]{:S(2)}) collective-permute-start(f32[16,128]{1,0:T(8,128)} %edges.1), channel_id=1, source_target_pairs={{0,1},{1,0},{2,3},{3,2},{4,5},{5,4},{6,7},{7,6},{8,9},{9,8},{10,11... | collective-permute-start | bytes 24584 | tf_op jit(solution)/shard_map/ppermute | solution.py:202
  17.8 4.7 %collective-permute-start.3 = (f32[16,128]{1,0:T(8,128)S(1)}, f32[16,128]{1,0:T(8,128)S(1)}, u32[]{:S(2)}, u32[]{:S(2)}) collective-permute-start(f32[16,128]{1,0:T(8,128)S(1)} %add.15), channel_id=1, source_target_pairs={{0,2},{1,3},{2,0},{3,1},{4,6},{5,7},{6,4},{7,5},{8,10},{9,11},{10,... | collective-permute-start | bytes 24584 | tf_op jit(solution)/shard_map/ppermute | solution.py:202
  22.5 4.7 %collective-permute-start.4 = (f32[16,128]{1,0:T(8,128)S(1)}, f32[16,128]{1,0:T(8,128)S(1)}, u32[]{:S(2)}, u32[]{:S(2)}) collective-permute-start(f32[16,128]{1,0:T(8,128)S(1)} %add.16), channel_id=1, source_target_pairs={{0,4},{1,5},{2,6},{3,7},{4,0},{5,1},{6,2},{7,3},{8,12},{9,13},{10,... | collective-permute-start | bytes 24584 | tf_op jit(solution)/shard_map/ppermute | solution.py:202
  27.2 4.3 %collective-permute-start.5 = (f32[16,128]{1,0:T(8,128)S(1)}, f32[16,128]{1,0:T(8,128)S(1)}, u32[]{:S(2)}, u32[]{:S(2)}) collective-permute-start(f32[16,128]{1,0:T(8,128)S(1)} %add.17), channel_id=1, source_target_pairs={{0,8},{8,0},{16,24},{24,16},{1,9},{9,1},{17,25},{25,17},{2,10},{10... | collective-permute-start | bytes 24584 | tf_op jit(solution)/shard_map/ppermute | solution.py:202
  31.5 4.9 %collective-permute-start.6 = (f32[16,128]{1,0:T(8,128)S(1)}, f32[16,128]{1,0:T(8,128)S(1)}, u32[]{:S(2)}, u32[]{:S(2)}) collective-permute-start(f32[16,128]{1,0:T(8,128)S(1)} %add.18), channel_id=1, source_target_pairs={{0,16},{8,24},{16,0},{24,8},{1,17},{9,25},{17,1},{25,9},{2,18},{10... | collective-permute-start | bytes 24584 | tf_op jit(solution)/shard_map/ppermute | solution.py:202

commit v2 on v1

v2 whole, which is shorter than its diff:
```python
import functools
import math

import jax
import jax.numpy as jnp
from jax import lax
from jax.experimental import pallas as pl
from jax.experimental.pallas import tpu as pltpu
from jax.sharding import PartitionSpec as P

ITERS = 2
TWO_PI = 2.0 * math.pi
CYCLE = 1.0 / TWO_PI
LANES = 128
VMEM_LIMIT = 32 * 2**20


def iota(shape, dim):
    return lax.broadcasted_iota(jnp.int32, shape, dim)


def wraps(change):
    return jnp.floor(change + 0.5)


def along(line):
    return jnp.where(iota(line.shape, 1) == 0, 0.0, wraps(line - pltpu.roll(line, 1, 1)))


def upper_ones(length, width):
    shape = (length, width)
    return (iota(shape, 0) - (length - width) <= iota(shape, 1)).astype(jnp.bfloat16)


def prefix_blocks(counts, ones, width):
    length = counts.shape[1]
    narrow = counts.astype(jnp.bfloat16)
    return [
        jnp.dot(narrow[:, :stop], ones[length - stop :, :], preferred_element_type=jnp.float32)
        for stop in range(width, length + 1, width)
    ]


def integrate_kernel(w_ref, u_ref, cols_ref, rows_ref, tile, sems, *, height, width):
    rows, length = tile.shape
    copies = []
    for step in range(rows // height):
        part = pl.ds(step * height, height)
        copies.append(pltpu.make_async_copy(w_ref.at[part], tile.at[part], sems.at[step]))
        copies[-1].start()
    ones = upper_ones(length, width)
    lower = (iota((height, height), 0) >= iota((height, height), 1)).astype(jnp.bfloat16)
    last_wraps = jnp.zeros((1, LANES), jnp.float32)
    last_phase = None
    for step, copy in enumerate(copies):
        copy.wait()
        part = slice(step * height, (step + 1) * height)
        phase = tile[part, :] * CYCLE
        edge = phase[:, :LANES]
        if last_phase is None:
            last_phase = edge[0:1, :]
        before = jnp.where(iota(edge.shape, 0) == 0, last_phase, pltpu.roll(edge, 1, 0))
        down = wraps(edge - before).astype(jnp.bfloat16)
        down = jnp.dot(lower, down, preferred_element_type=jnp.float32) + last_wraps
        last_phase, last_wraps = edge[height - 1 :, :], down[height - 1 :, :]
        first = down[:, 0:1]
        blocks = prefix_blocks(along(phase), ones, width)
        for n, block in enumerate(blocks):
            span = slice(n * width, (n + 1) * width)
            total = first + block
            u_ref[part, span] = phase[:, span] - total
            if step == len(copies) - 1:
                rows_ref[0:1, span] = total[height - 1 :, :]
        cols_ref[0:1, part] = total[:, width - LANES :].T[LANES - 1 :, :]
        cols_ref[1:3, part] = phase[:, length - LANES :].T[LANES - 2 :, :]
    rows_ref[1:3, :] = phase[height - 2 :, :]


def side_sums(lines, halo, cycles, at_end, width):
    total, inner, outer = lines[0:1, :], lines[1:2, :], lines[2:3, :]
    lane = iota(total.shape, 1)
    length = total.shape[1]
    outer_wraps, halo_wraps = along(outer), along(halo)
    cross = wraps(outer - inner)
    charge = along(inner) + cross - outer_wraps - pltpu.roll(cross, 1, 1)
    weight = jnp.where(lane == 0, 0.0, 1.0 / (1.0 + jnp.abs(charge)))
    beyond = wraps(halo - outer)
    next_charge = outer_wraps + beyond - halo_wraps - pltpu.roll(beyond, 1, 1)
    next_weight = 1.0 / (1.0 + jnp.abs(next_charge))
    ones = upper_ones(length, width)
    halo_total = jnp.concatenate(
        [b[0:1, :] for b in prefix_blocks(jnp.broadcast_to(halo_wraps, (8, length)), ones, width)],
        axis=1,
    )
    jump = jnp.where(at_end, outer - total, halo_total - total - beyond) + cycles

    def add(values):
        return jnp.sum(values, axis=1, keepdims=True)

    return [
        add(weight * jump),
        add(weight),
        add(jnp.where(lane == 0, jump, 0.0)),
        add(jnp.where(lane == length - 1, next_weight, 0.0)),
    ]


def edges_kernel(
    right_steps, down_steps, cols_ref, rows_ref, right_ref, below_ref, table_ref, *, grid, widths
):
    row, col = lax.axis_index("row"), lax.axis_index("col")
    values = side_sums(cols_ref[...], right_ref[...] * CYCLE, right_steps[0, 0, 0].astype(jnp.float32), col == grid[1] - 1, widths[0])
    values += side_sums(rows_ref[...], below_ref[...] * CYCLE, down_steps[0, 0, 0].astype(jnp.float32), row == grid[0] - 1, widths[1])
    shape = table_ref.shape
    table = jnp.zeros(shape, jnp.float32)
    for n, value in enumerate(values):
        table = jnp.where(iota(shape, 0) == n, value, table)
    table_ref[...] = jnp.where(iota(shape, 1) == row * grid[1] + col, table, 0.0)


def tile_offsets(table, grid):
    tile_rows, tile_cols = grid
    shape = (8, table.shape[1])
    size = table.shape[1]
    lane = iota(shape, 1)
    r, c = lane // tile_cols, lane % tile_cols
    there = lane < tile_rows * tile_cols

    def line(n):
        return jnp.broadcast_to(table[n : n + 1, :], shape)

    first = jnp.where(r == 0, 1.0, pltpu.roll(line(7), tile_cols, 1))
    across = (line(0) + first * line(2)) / (line(1) + first)
    across = jnp.where(there, across, 0.0)
    first = jnp.where(c == 0, 1.0, pltpu.roll(line(3), 1, 1))
    down = (line(4) + first * line(6)) / (line(5) + first)
    down = jnp.where(there, down, 0.0)
    source, target = iota((size, size), 0), iota((size, size), 1)
    sr, sc = source // tile_cols, source % tile_cols
    tr, tc = target // tile_cols, target % tile_cols
    use_across = jnp.where(sc < tc, 0.5, 0.0)
    use_across = jnp.where(sr == tr, use_across, 0.0) + jnp.where(sr == 0, use_across, 0.0)
    use_down = jnp.where(sr < tr, 0.5, 0.0)
    use_down = jnp.where(sc == tc, use_down, 0.0) + jnp.where(sc == 0, use_down, 0.0)
    dot = functools.partial(
        jnp.dot, precision=lax.Precision.HIGHEST, preferred_element_type=jnp.float32
    )
    totals = jnp.zeros(shape, jnp.float32)
    for _ in range(ITERS):
        right = jnp.where(c == tile_cols - 1, 0.0, pltpu.roll(totals, size - 1, 1))
        below = jnp.where(r == tile_rows - 1, 0.0, pltpu.roll(totals, size - tile_cols, 1))
        horizontal = across + totals - right
        vertical = down + totals - below
        step = dot(horizontal, use_across) + dot(vertical, use_down)
        totals = totals + jnp.where(there, step, 0.0)
    return totals


def shift_kernel(mine_ref, theirs_ref, u_ref, out_ref, moved, sems, *, grid, height):
    totals = tile_offsets(mine_ref[...] + theirs_ref[...], grid)[0:1, :]
    me = lax.axis_index("row") * grid[1] + lax.axis_index("col")
    offset = jnp.sum(jnp.where(iota(totals.shape, 1) == me, totals, 0.0), axis=1, keepdims=True)
    copies = []
    for step in range(u_ref.shape[0] // height):
        part = pl.ds(step * height, height)
        moved[part, :] = u_ref[part, :] + offset
        copies.append(pltpu.make_async_copy(moved.at[part], out_ref.at[part], sems.at[step]))
        copies[-1].start()
    for copy in copies:
        copy.wait()


def integrate(tile):
    rows, cols = tile.shape
    height, width = math.gcd(rows, 256), math.gcd(cols, 256)
    vmem = pl.BlockSpec(memory_space=pltpu.VMEM)
    return pl.pallas_call(
        functools.partial(integrate_kernel, height=height, width=width),
        in_specs=[pl.BlockSpec(memory_space=pltpu.HBM)],
        out_specs=[vmem, vmem, vmem],
        out_shape=[
            pltpu.VMEM((rows, cols), jnp.float32),
            pltpu.VMEM((8, rows), jnp.float32),
            pltpu.VMEM((8, cols), jnp.float32),
        ],
        scratch_shapes=[
            pltpu.VMEM((rows, cols), jnp.float32),
            pltpu.SemaphoreType.DMA((rows // height,)),
        ],
        compiler_params=pltpu.CompilerParams(vmem_limit_bytes=VMEM_LIMIT),
            name="integrate",
    )(pltpu.with_memory_space_constraint(tile, pltpu.HBM))


def near(array):
    return pltpu.with_memory_space_constraint(array, pltpu.VMEM)


def gathered(table, grid):
    theirs = jnp.zeros_like(table)
    for axis, count in zip(("col", "row"), grid[::-1]):
        if count & (count - 1):
            table, theirs = lax.psum(table + theirs, axis), jnp.zeros_like(table)
            continue
        bit = 1
        while bit < count:
            table = table + theirs
            theirs = lax.ppermute(table, axis, [(i, i ^ bit) for i in range(count)])
            bit *= 2
    return near(table), near(theirs)


def on_device(grid, wrapped, col_steps, row_steps):
    frames, rows, cols = wrapped.shape
    widths = (math.gcd(rows, 256), math.gcd(cols, 256))
    slots = -(-grid[0] * grid[1] // LANES) * LANES
    smem = pl.BlockSpec(memory_space=pltpu.SMEM)
    vmem = pl.BlockSpec(memory_space=pltpu.VMEM)
    outs = []
    for f in range(frames):
        tile = wrapped[f]
        right = lax.ppermute(tile[:, 0][None, :], "col", [(i + 1, i) for i in range(grid[1] - 1)])
        below = lax.ppermute(tile[0:1, :], "row", [(i + 1, i) for i in range(grid[0] - 1)])
        cycles, col_lines, row_lines = integrate(tile)
        table = pl.pallas_call(
            functools.partial(edges_kernel, grid=grid, widths=widths),
            in_specs=[smem, smem, vmem, vmem, vmem, vmem],
            out_specs=vmem,
            out_shape=pltpu.VMEM((8, slots), jnp.float32),
            compiler_params=pltpu.CompilerParams(vmem_limit_bytes=VMEM_LIMIT),
            name="edges",
        )(
            col_steps[f : f + 1], row_steps[f : f + 1], near(col_lines), near(row_lines), near(right), near(below)
        )
        mine, theirs = gathered(table, grid)
        height = math.gcd(rows, 128)
        outs.append(
            pl.pallas_call(
                functools.partial(shift_kernel, grid=grid, height=height),
                in_specs=[vmem, vmem, vmem],
                out_specs=pl.BlockSpec(memory_space=pl.ANY),
                out_shape=jax.ShapeDtypeStruct((rows, cols), jnp.float32),
                scratch_shapes=[
                    pltpu.VMEM((rows, cols), jnp.float32),
                    pltpu.SemaphoreType.DMA((rows // height,)),
                ],
                compiler_params=pltpu.CompilerParams(vmem_limit_bytes=VMEM_LIMIT),
            name="shift",
            )(mine, theirs, near(cycles))
        )
    return jnp.stack(outs)


def solution(mesh):
    grid = (mesh.shape["row"], mesh.shape["col"])
    spec = P(None, "row", "col")
    return jax.shard_map(
        functools.partial(on_device, grid),
        mesh=mesh,
        in_specs=(spec, spec, spec),
        out_specs=spec,
        check_vma=False,
    )
```

time: 43.1 us -> 34.6 us (0.80)
  Pallas kernels: 14.1 us -> 8.09 us
  other arithmetic: 1.3 us -> 0.01 us
  local copies, waits for them, and re-layouts: 2.59 us -> 2.01 us
    pallas_call x2, Pallas kernels: 12.1 us -> 7.49 us  [the longest x1 4.55 us: integrate(): pl.pallas_call(functools.partial(integrate_kernel, height=height, width=w...]
    pallas_call x1, Pallas kernels: 1.97 us -> 0.6 us  [on_device(): pl.pallas_call(functools.partial(edges_kernel, grid=grid, widths=widths),...]
    add x5 -> x4, other arithmetic: 1.3 us -> 0.01 us  [gathered(): table = table + theirs]
    unnamed x4 -> x0, local copies, waits for them, and re-layouts: 0.58 us -> none
  transfers between devices with their start and end apart: 7 -> 7, of which waited for: 5 -> 5; matrix products, arithmetic and copies ran while one was open for 3% -> 4% of each run, Pallas kernels for 15% -> 13%
where the time goes in v2:
time: 34.6 us; the launch traced here: 34.3 us
  starting transfers between devices  15.7 us (45%)
  Pallas kernels  8.09 us (23%)
  waiting for transfers between devices  7.16 us (21%)
  local copies, waits for them, and re-layouts  2.01 us (6%)
  between operations  1.35 us (4%)
    ppermute x5, starting transfers between devices, gathered(): theirs = lax.ppermute(table, axis, [(i, i ^ bit) for i in range(count)])  13.1 us
    ppermute x5, waiting for transfers between devices, gathered(): theirs = lax.ppermute(table, axis, [(i, i ^ bit) for i in range(count)])  7.16 us
    pallas_call x1, Pallas kernels, integrate(): pl.pallas_call(functools.partial(integrate_kernel, height=height, width=w...  4.55 us
    pallas_call x1, Pallas kernels, on_device(): pl.pallas_call(functools.partial(shift_kernel, grid=grid, height=height),...  2.94 us
    ppermute x1, starting transfers between devices, on_device(): lax.ppermute(tile[:, 0][None, :], 'col', [(i + 1, i) for i in range(grid[...  1.29 us
    ppermute x1, starting transfers between devices, on_device(): lax.ppermute(tile[0:1, :], 'row', [(i + 1, i) for i in range(grid[0] - 1)])  1.28 us
    slice x1, local copies, waits for them, and re-layouts, on_device(): tile[:, 0][None, :]  1.25 us
    slice x1, local copies, waits for them, and re-layouts, on_device(): tile[0:1, :]  0.76 us
  transfers between devices with their start and end apart: 7, of which 5 were waited for; matrix products, arithmetic and copies ran while one was open for 4% of the time, Pallas kernels for 13%

profile of v2, /device:TPU:0, one launch (start us, length us, event | category | flops | bytes accessed | tf_op | source)
XLA Modules:
  0.0 34.3 jit_solution(9081814124808713865)
XLA Ops:
  0.0 0.8 %slice_bitcast_fusion = f32[1,1024]{1,0:T(1,128)S(1)} fusion(f32[1,1024,1024]{2,1,0:T(8,128)} %param.3), kind=kLoop, calls=%fused_computation.1 | loop fusion | bytes 8192 | tf_op jit(solution)/shard_map/slice | solution.py:223
  0.8 1.3 %collective-permute-start.1 = (f32[1,1024]{1,0:T(1,128)S(1)}, f32[1,1024]{1,0:T(1,128)S(1)}, u32[]{:S(2)}, u32[]{:S(2)}) collective-permute-start(f32[1,1024]{1,0:T(1,128)S(1)} %slice_bitcast_fusion), channel_id=1, source_target_pairs={{8,0},{16,8},{24,16},{9,1},{17,9},{25,17},{10,2},{18,10},{26,18},{... | collective-permute-start | bytes 12296 | tf_op jit(solution)/shard_map/ppermute | solution.py:223
  2.0 1.2 %slice_reduce_fusion = f32[1024]{0:T(1024)S(1)} fusion(f32[1024,1024]{1,0:T(8,128)} %bitcast.5), kind=kLoop, calls=%fused_computation | loop fusion | bytes 8192 | tf_op jit(solution)/shard_map/slice | solution.py:222
  3.3 1.3 %collective-permute-start = (f32[1,1024]{1,0:T(1,128)S(1)}, f32[1,1024]{1,0:T(1,128)S(1)}, u32[]{:S(2)}, u32[]{:S(2)}) collective-permute-start(f32[1,1024]{1,0:T(1,128)S(1)} %bitcast.7), channel_id=1, source_target_pairs={{1,0},{2,1},{3,2},{4,3},{5,4},{6,5},{7,6},{9,8},{10,9},{11,10},{12... | collective-permute-start | bytes 12296 | tf_op jit(solution)/shard_map/ppermute | solution.py:222
  4.6 4.6 %integrate.1 = (f32[1024,1024]{1,0:T(8,128)S(1)}, f32[8,1024]{1,0:T(8,128)S(1)}, f32[8,1024]{1,0:T(8,128)S(1)}) custom-call(f32[1024,1024]{1,0:T(8,128)} %bitcast.6), custom_call_target="tpu_custom_call" | custom-call | tf_op jit(solution)/shard_map/integrate/pallas_call | solution.py:177
  10.5 0.0 collective-permute-done.1.below_ref
  10.5 0.0 collective-permute-done.right_ref
  10.5 0.6 %edges.1 = f32[8,128]{1,0:T(8,128)S(1)} custom-call(s32[1,1,1]{2,1,0:T(1,128)S(6)} %copy.4.right_steps, s32[1,1,1]{2,1,0:T(1,128)S(6)} %copy.5.down_steps, f32[8,1024]{1,0:T(8,128)S(1)} %get-tuple-element.8.cols_ref, f32[8,1024]{1,0:T(8,128)S(1)} %get-tuple-element.9.rows_ref, f32[1,1024]{1,0:T(1,128)S(1)} %collective-permute-done.right_ref, ...), custom_call_target="tpu_custom_call" | custom-call | tf_op jit(solution)/shard_map/edges/pallas_call | solution.py:225
  11.1 1.1 %collective-permute-start.2 = (f32[8,128]{1,0:T(8,128)S(1)}, f32[8,128]{1,0:T(8,128)S(1)}, u32[]{:S(2)}, u32[]{:S(2)}) collective-permute-start(f32[8,128]{1,0:T(8,128)S(1)} %edges.1), channel_id=1, source_target_pairs={{0,1},{1,0},{2,3},{3,2},{4,5},{5,4},{6,7},{7,6},{8,9},{9,8},{10,11... | collective-permute-start | bytes 12296 | tf_op jit(solution)/shard_map/ppermute | solution.py:208
  12.2 0.8 %collective-permute-done.2 = f32[8,128]{1,0:T(8,128)S(1)} collective-permute-done((f32[8,128]{1,0:T(8,128)S(1)}, f32[8,128]{1,0:T(8,128)S(1)}, u32[]{:S(2)}, u32[]{:S(2)}) %collective-permute-start.2) | collective-permute-done | bytes 4128 | tf_op jit(solution)/shard_map/ppermute | solution.py:208
  13.0 3.1 %collective-permute-start.3 = (f32[8,128]{1,0:T(8,128)S(1)}, f32[8,128]{1,0:T(8,128)S(1)}, u32[]{:S(2)}, u32[]{:S(2)}) collective-permute-start(f32[8,128]{1,0:T(8,128)S(1)} %add.12), channel_id=1, source_target_pairs={{0,2},{1,3},{2,0},{3,1},{4,6},{5,7},{6,4},{7,5},{8,10},{9,11},{10,... | collective-permute-start | bytes 12296 | tf_op jit(solution)/shard_map/ppermute | solution.py:208
  16.1 1.6 %collective-permute-done.3 = f32[8,128]{1,0:T(8,128)S(1)} collective-permute-done((f32[8,128]{1,0:T(8,128)S(1)}, f32[8,128]{1,0:T(8,128)S(1)}, u32[]{:S(2)}, u32[]{:S(2)}) %collective-permute-start.3) | collective-permute-done | bytes 4128 | tf_op jit(solution)/shard_map/ppermute | solution.py:208
  17.7 3.0 %collective-permute-start.4 = (f32[8,128]{1,0:T(8,128)S(1)}, f32[8,128]{1,0:T(8,128)S(1)}, u32[]{:S(2)}, u32[]{:S(2)}) collective-permute-start(f32[8,128]{1,0:T(8,128)S(1)} %add.13), channel_id=1, source_target_pairs={{0,4},{1,5},{2,6},{3,7},{4,0},{5,1},{6,2},{7,3},{8,12},{9,13},{10,... | collective-permute-start | bytes 12296 | tf_op jit(solution)/shard_map/ppermute | solution.py:208
  20.7 1.6 %collective-permute-done.4 = f32[8,128]{1,0:T(8,128)S(1)} collective-permute-done((f32[8,128]{1,0:T(8,128)S(1)}, f32[8,128]{1,0:T(8,128)S(1)}, u32[]{:S(2)}, u32[]{:S(2)}) %collective-permute-start.4) | collective-permute-done | bytes 4128 | tf_op jit(solution)/shard_map/ppermute | solution.py:208
  22.3 2.6 %collective-permute-start.5 = (f32[8,128]{1,0:T(8,128)S(1)}, f32[8,128]{1,0:T(8,128)S(1)}, u32[]{:S(2)}, u32[]{:S(2)}) collective-permute-start(f32[8,128]{1,0:T(8,128)S(1)} %add.14), channel_id=1, source_target_pairs={{0,8},{8,0},{16,24},{24,16},{1,9},{9,1},{17,25},{25,17},{2,10},{10... | collective-permute-start | bytes 12296 | tf_op jit(solution)/shard_map/ppermute | solution.py:208
  24.9 1.6 %collective-permute-done.5 = f32[8,128]{1,0:T(8,128)S(1)} collective-permute-done((f32[8,128]{1,0:T(8,128)S(1)}, f32[8,128]{1,0:T(8,128)S(1)}, u32[]{:S(2)}, u32[]{:S(2)}) %collective-permute-start.5) | collective-permute-done | bytes 4128 | tf_op jit(solution)/shard_map/ppermute | solution.py:208
  26.5 3.3 %collective-permute-start.6 = (f32[8,128]{1,0:T(8,128)S(1)}, f32[8,128]{1,0:T(8,128)S(1)}, u32[]{:S(2)}, u32[]{:S(2)}) collective-permute-start(f32[8,128]{1,0:T(8,128)S(1)} %add.15.mine_ref), channel_id=1, source_target_pairs={{0,16},{8,24},{16,0},{24,8},{1,17},{9,25},{17,1},{25,9},{2,18},{10... | collective-permute-start | bytes 12296 | tf_op jit(solution)/shard_map/ppermute | solution.py:208
  29.8 1.6 %collective-permute-done.6.theirs_ref = f32[8,128]{1,0:T(8,128)S(1)} collective-permute-done((f32[8,128]{1,0:T(8,128)S(1)}, f32[8,128]{1,0:T(8,128)S(1)}, u32[]{:S(2)}, u32[]{:S(2)}) %collective-permute-start.6) | collective-permute-done | bytes 4128 | tf_op jit(solution)/shard_map/ppermute | solution.py:208
  31.4 2.9 %shift.1 = f32[1024,1024]{1,0:T(8,128)} custom-call(f32[8,128]{1,0:T(8,128)S(1)} %add.15.mine_ref, f32[8,128]{1,0:T(8,128)S(1)} %collective-permute-done.6.theirs_ref, f32[1024,1024]{1,0:T(8,128)S(1)} %get-tuple-element.10.u_ref), custom_call_target="tpu_custom_call" | custom-call | tf_op jit(solution)/shard_map/shift/pallas_call | solution.py:238
  (4 shorter events, 0.0 us)
Async XLA Ops:
  0.8 9.7 %collective-permute-start.1 = (f32[1,1024]{1,0:T(1,128)S(1)}, f32[1,1024]{1,0:T(1,128)S(1)}, u32[]{:S(2)}, u32[]{:S(2)}) collective-permute-start(f32[1,1024]{1,0:T(1,128)S(1)} %slice_bitcast_fusion), channel_id=1, source_target_pairs={{8,0},{16,8},{24,16},{9,1},{17,9},{25,17},{10,2},{18,10},{26,18},{... | collective-permute-start | bytes 12296 | tf_op jit(solution)/shard_map/ppermute | solution.py:223
  3.3 7.2 %collective-permute-start = (f32[1,1024]{1,0:T(1,128)S(1)}, f32[1,1024]{1,0:T(1,128)S(1)}, u32[]{:S(2)}, u32[]{:S(2)}) collective-permute-start(f32[1,1024]{1,0:T(1,128)S(1)} %bitcast.7), channel_id=1, source_target_pairs={{1,0},{2,1},{3,2},{4,3},{5,4},{6,5},{7,6},{9,8},{10,9},{11,10},{12... | collective-permute-start | bytes 12296 | tf_op jit(solution)/shard_map/ppermute | solution.py:222
  11.1 2.0 %collective-permute-start.2 = (f32[8,128]{1,0:T(8,128)S(1)}, f32[8,128]{1,0:T(8,128)S(1)}, u32[]{:S(2)}, u32[]{:S(2)}) collective-permute-start(f32[8,128]{1,0:T(8,128)S(1)} %edges.1), channel_id=1, source_target_pairs={{0,1},{1,0},{2,3},{3,2},{4,5},{5,4},{6,7},{7,6},{8,9},{9,8},{10,11... | collective-permute-start | bytes 12296 | tf_op jit(solution)/shard_map/ppermute | solution.py:208
  13.0 4.6 %collective-permute-start.3 = (f32[8,128]{1,0:T(8,128)S(1)}, f32[8,128]{1,0:T(8,128)S(1)}, u32[]{:S(2)}, u32[]{:S(2)}) collective-permute-start(f32[8,128]{1,0:T(8,128)S(1)} %add.12), channel_id=1, source_target_pairs={{0,2},{1,3},{2,0},{3,1},{4,6},{5,7},{6,4},{7,5},{8,10},{9,11},{10,... | collective-permute-start | bytes 12296 | tf_op jit(solution)/shard_map/ppermute | solution.py:208
  17.7 4.6 %collective-permute-start.4 = (f32[8,128]{1,0:T(8,128)S(1)}, f32[8,128]{1,0:T(8,128)S(1)}, u32[]{:S(2)}, u32[]{:S(2)}) collective-permute-start(f32[8,128]{1,0:T(8,128)S(1)} %add.13), channel_id=1, source_target_pairs={{0,4},{1,5},{2,6},{3,7},{4,0},{5,1},{6,2},{7,3},{8,12},{9,13},{10,... | collective-permute-start | bytes 12296 | tf_op jit(solution)/shard_map/ppermute | solution.py:208
  22.3 4.2 %collective-permute-start.5 = (f32[8,128]{1,0:T(8,128)S(1)}, f32[8,128]{1,0:T(8,128)S(1)}, u32[]{:S(2)}, u32[]{:S(2)}) collective-permute-start(f32[8,128]{1,0:T(8,128)S(1)} %add.14), channel_id=1, source_target_pairs={{0,8},{8,0},{16,24},{24,16},{1,9},{9,1},{17,25},{25,17},{2,10},{10... | collective-permute-start | bytes 12296 | tf_op jit(solution)/shard_map/ppermute | solution.py:208
  26.5 4.9 %collective-permute-start.6 = (f32[8,128]{1,0:T(8,128)S(1)}, f32[8,128]{1,0:T(8,128)S(1)}, u32[]{:S(2)}, u32[]{:S(2)}) collective-permute-start(f32[8,128]{1,0:T(8,128)S(1)} %add.15.mine_ref), channel_id=1, source_target_pairs={{0,16},{8,24},{16,0},{24,8},{1,17},{9,25},{17,1},{25,9},{2,18},{10... | collective-permute-start | bytes 12296 | tf_op jit(solution)/shard_map/ppermute | solution.py:208

commit v3 on v2

--- a/solution.py
+++ b/solution.py
@@ -172,7 +172,7 @@
 
 def integrate(tile):
     rows, cols = tile.shape
-    height, width = math.gcd(rows, 256), math.gcd(cols, 256)
+    height, width = math.gcd(rows, 512), math.gcd(cols, 256)
     vmem = pl.BlockSpec(memory_space=pltpu.VMEM)
     return pl.pallas_call(
         functools.partial(integrate_kernel, height=height, width=width),
@@ -198,15 +198,15 @@
 
 def gathered(table, grid):
     theirs = jnp.zeros_like(table)
-    for axis, count in zip(("col", "row"), grid[::-1]):
+    for axis, count in zip(("row", "col"), grid):
         if count & (count - 1):
             table, theirs = lax.psum(table + theirs, axis), jnp.zeros_like(table)
             continue
-        bit = 1
-        while bit < count:
+        bit = count // 2
+        while bit:
             table = table + theirs
             theirs = lax.ppermute(table, axis, [(i, i ^ bit) for i in range(count)])
-            bit *= 2
+            bit //= 2
     return near(table), near(theirs)
 
 

time: 34.6 us -> 33.7 us (0.974)
  starting transfers between devices: 15.7 us -> 13.3 us
  waiting for transfers between devices: 7.16 us -> 9.05 us
  Pallas kernels: 8.09 us -> 7.66 us
    ppermute x5, starting transfers between devices: 13.1 us -> 10.8 us  [gathered(): theirs = lax.ppermute(table, axis, [(i, i ^ bit) for i in range(count)])]
    ppermute x5, waiting for transfers between devices: 7.16 us -> 9.05 us  [gathered(): theirs = lax.ppermute(table, axis, [(i, i ^ bit) for i in range(count)])]
    pallas_call x1, Pallas kernels: 4.55 us -> 4.13 us  [integrate(): pl.pallas_call(functools.partial(integrate_kernel, height=height, width=w...]
  transfers between devices with their start and end apart: 7 -> 7, of which waited for: 5 -> 5; matrix products, arithmetic and copies ran while one was open for 4% -> 4% of each run, Pallas kernels for 13% -> 12%
where the time goes in v3:
time: 33.7 us; the launch traced here: 33.4 us
  starting transfers between devices  13.3 us (39%)
  waiting for transfers between devices  9.05 us (27%)
  Pallas kernels  7.66 us (23%)
  local copies, waits for them, and re-layouts  2.01 us (6%)
  between operations  1.35 us (4%)
    ppermute x5, starting transfers between devices, gathered(): theirs = lax.ppermute(table, axis, [(i, i ^ bit) for i in range(count)])  10.8 us
    ppermute x5, waiting for transfers between devices, gathered(): theirs = lax.ppermute(table, axis, [(i, i ^ bit) for i in range(count)])  9.05 us
    pallas_call x1, Pallas kernels, integrate(): pl.pallas_call(functools.partial(integrate_kernel, height=height, width=w...  4.13 us
    pallas_call x1, Pallas kernels, on_device(): pl.pallas_call(functools.partial(shift_kernel, grid=grid, height=height),...  2.94 us
    ppermute x1, starting transfers between devices, on_device(): lax.ppermute(tile[:, 0][None, :], 'col', [(i + 1, i) for i in range(grid[...  1.29 us
    ppermute x1, starting transfers between devices, on_device(): lax.ppermute(tile[0:1, :], 'row', [(i + 1, i) for i in range(grid[0] - 1)])  1.28 us
    slice x1, local copies, waits for them, and re-layouts, on_device(): tile[:, 0][None, :]  1.25 us
    slice x1, local copies, waits for them, and re-layouts, on_device(): tile[0:1, :]  0.76 us
  transfers between devices with their start and end apart: 7, of which 5 were waited for; matrix products, arithmetic and copies ran while one was open for 4% of the time, Pallas kernels for 12%

profile of v3, /device:TPU:0, one launch (start us, length us, event | category | flops | bytes accessed | tf_op | source)
XLA Modules:
  0.0 33.4 jit_solution(7875051165269252502)
XLA Ops:
  0.0 0.8 %slice_bitcast_fusion = f32[1,1024]{1,0:T(1,128)S(1)} fusion(f32[1,1024,1024]{2,1,0:T(8,128)} %param.3), kind=kLoop, calls=%fused_computation.1 | loop fusion | bytes 8192 | tf_op jit(solution)/shard_map/slice | solution.py:223
  0.8 1.3 %collective-permute-start.1 = (f32[1,1024]{1,0:T(1,128)S(1)}, f32[1,1024]{1,0:T(1,128)S(1)}, u32[]{:S(2)}, u32[]{:S(2)}) collective-permute-start(f32[1,1024]{1,0:T(1,128)S(1)} %slice_bitcast_fusion), channel_id=1, source_target_pairs={{8,0},{16,8},{24,16},{9,1},{17,9},{25,17},{10,2},{18,10},{26,18},{... | collective-permute-start | bytes 12296 | tf_op jit(solution)/shard_map/ppermute | solution.py:223
  2.0 1.2 %slice_reduce_fusion = f32[1024]{0:T(1024)S(1)} fusion(f32[1024,1024]{1,0:T(8,128)} %bitcast.5), kind=kLoop, calls=%fused_computation | loop fusion | bytes 8192 | tf_op jit(solution)/shard_map/slice | solution.py:222
  3.3 1.3 %collective-permute-start = (f32[1,1024]{1,0:T(1,128)S(1)}, f32[1,1024]{1,0:T(1,128)S(1)}, u32[]{:S(2)}, u32[]{:S(2)}) collective-permute-start(f32[1,1024]{1,0:T(1,128)S(1)} %bitcast.7), channel_id=1, source_target_pairs={{1,0},{2,1},{3,2},{4,3},{5,4},{6,5},{7,6},{9,8},{10,9},{11,10},{12... | collective-permute-start | bytes 12296 | tf_op jit(solution)/shard_map/ppermute | solution.py:222
  4.6 4.1 %integrate.1 = (f32[1024,1024]{1,0:T(8,128)S(1)}, f32[8,1024]{1,0:T(8,128)S(1)}, f32[8,1024]{1,0:T(8,128)S(1)}) custom-call(f32[1024,1024]{1,0:T(8,128)} %bitcast.6), custom_call_target="tpu_custom_call" | custom-call | tf_op jit(solution)/shard_map/integrate/pallas_call | solution.py:177
  10.0 0.0 collective-permute-done.1.below_ref
  10.0 0.0 collective-permute-done.right_ref
  10.1 0.6 %edges.1 = f32[8,128]{1,0:T(8,128)S(1)} custom-call(s32[1,1,1]{2,1,0:T(1,128)S(6)} %copy.4.right_steps, s32[1,1,1]{2,1,0:T(1,128)S(6)} %copy.5.down_steps, f32[8,1024]{1,0:T(8,128)S(1)} %get-tuple-element.8.cols_ref, f32[8,1024]{1,0:T(8,128)S(1)} %get-tuple-element.9.rows_ref, f32[1,1024]{1,0:T(1,128)S(1)} %collective-permute-done.right_ref, ...), custom_call_target="tpu_custom_call" | custom-call | tf_op jit(solution)/shard_map/edges/pallas_call | solution.py:225
  10.6 5.0 %collective-permute-start.2 = (f32[8,128]{1,0:T(8,128)S(1)}, f32[8,128]{1,0:T(8,128)S(1)}, u32[]{:S(2)}, u32[]{:S(2)}) collective-permute-start(f32[8,128]{1,0:T(8,128)S(1)} %edges.1), channel_id=1, source_target_pairs={{0,16},{8,24},{16,0},{24,8},{1,17},{9,25},{17,1},{25,9},{2,18},{10... | collective-permute-start | bytes 12296 | tf_op jit(solution)/shard_map/ppermute | solution.py:208
  15.7 1.6 %collective-permute-done.2 = f32[8,128]{1,0:T(8,128)S(1)} collective-permute-done((f32[8,128]{1,0:T(8,128)S(1)}, f32[8,128]{1,0:T(8,128)S(1)}, u32[]{:S(2)}, u32[]{:S(2)}) %collective-permute-start.2) | collective-permute-done | bytes 4128 | tf_op jit(solution)/shard_map/ppermute | solution.py:208
  17.3 0.6 %collective-permute-start.3 = (f32[8,128]{1,0:T(8,128)S(1)}, f32[8,128]{1,0:T(8,128)S(1)}, u32[]{:S(2)}, u32[]{:S(2)}) collective-permute-start(f32[8,128]{1,0:T(8,128)S(1)} %add.12), channel_id=1, source_target_pairs={{0,8},{8,0},{16,24},{24,16},{1,9},{9,1},{17,25},{25,17},{2,10},{10... | collective-permute-start | bytes 12296 | tf_op jit(solution)/shard_map/ppermute | solution.py:208
  17.9 3.0 %collective-permute-done.3 = f32[8,128]{1,0:T(8,128)S(1)} collective-permute-done((f32[8,128]{1,0:T(8,128)S(1)}, f32[8,128]{1,0:T(8,128)S(1)}, u32[]{:S(2)}, u32[]{:S(2)}) %collective-permute-start.3) | collective-permute-done | bytes 4128 | tf_op jit(solution)/shard_map/ppermute | solution.py:208
  20.9 3.2 %collective-permute-start.4 = (f32[8,128]{1,0:T(8,128)S(1)}, f32[8,128]{1,0:T(8,128)S(1)}, u32[]{:S(2)}, u32[]{:S(2)}) collective-permute-start(f32[8,128]{1,0:T(8,128)S(1)} %add.13), channel_id=1, source_target_pairs={{0,4},{1,5},{2,6},{3,7},{4,0},{5,1},{6,2},{7,3},{8,12},{9,13},{10,... | collective-permute-start | bytes 12296 | tf_op jit(solution)/shard_map/ppermute | solution.py:208
  24.1 1.6 %collective-permute-done.4 = f32[8,128]{1,0:T(8,128)S(1)} collective-permute-done((f32[8,128]{1,0:T(8,128)S(1)}, f32[8,128]{1,0:T(8,128)S(1)}, u32[]{:S(2)}, u32[]{:S(2)}) %collective-permute-start.4) | collective-permute-done | bytes 4128 | tf_op jit(solution)/shard_map/ppermute | solution.py:208
  25.7 1.9 %collective-permute-start.5 = (f32[8,128]{1,0:T(8,128)S(1)}, f32[8,128]{1,0:T(8,128)S(1)}, u32[]{:S(2)}, u32[]{:S(2)}) collective-permute-start(f32[8,128]{1,0:T(8,128)S(1)} %add.14), channel_id=1, source_target_pairs={{0,2},{1,3},{2,0},{3,1},{4,6},{5,7},{6,4},{7,5},{8,10},{9,11},{10,... | collective-permute-start | bytes 12296 | tf_op jit(solution)/shard_map/ppermute | solution.py:208
  27.6 1.7 %collective-permute-done.5 = f32[8,128]{1,0:T(8,128)S(1)} collective-permute-done((f32[8,128]{1,0:T(8,128)S(1)}, f32[8,128]{1,0:T(8,128)S(1)}, u32[]{:S(2)}, u32[]{:S(2)}) %collective-permute-start.5) | collective-permute-done | bytes 4128 | tf_op jit(solution)/shard_map/ppermute | solution.py:208
  29.3 0.0 collective-permute-start.6
  29.3 1.2 %collective-permute-done.6.theirs_ref = f32[8,128]{1,0:T(8,128)S(1)} collective-permute-done((f32[8,128]{1,0:T(8,128)S(1)}, f32[8,128]{1,0:T(8,128)S(1)}, u32[]{:S(2)}, u32[]{:S(2)}) %collective-permute-start.6) | collective-permute-done | bytes 4128 | tf_op jit(solution)/shard_map/ppermute | solution.py:208
  30.5 2.9 %shift.1 = f32[1024,1024]{1,0:T(8,128)} custom-call(f32[8,128]{1,0:T(8,128)S(1)} %add.15.mine_ref, f32[8,128]{1,0:T(8,128)S(1)} %collective-permute-done.6.theirs_ref, f32[1024,1024]{1,0:T(8,128)S(1)} %get-tuple-element.10.u_ref), custom_call_target="tpu_custom_call" | custom-call | tf_op jit(solution)/shard_map/shift/pallas_call | solution.py:238
  (4 shorter events, 0.0 us)
Async XLA Ops:
  0.8 9.3 %collective-permute-start.1 = (f32[1,1024]{1,0:T(1,128)S(1)}, f32[1,1024]{1,0:T(1,128)S(1)}, u32[]{:S(2)}, u32[]{:S(2)}) collective-permute-start(f32[1,1024]{1,0:T(1,128)S(1)} %slice_bitcast_fusion), channel_id=1, source_target_pairs={{8,0},{16,8},{24,16},{9,1},{17,9},{25,17},{10,2},{18,10},{26,18},{... | collective-permute-start | bytes 12296 | tf_op jit(solution)/shard_map/ppermute | solution.py:223
  3.3 6.7 %collective-permute-start = (f32[1,1024]{1,0:T(1,128)S(1)}, f32[1,1024]{1,0:T(1,128)S(1)}, u32[]{:S(2)}, u32[]{:S(2)}) collective-permute-start(f32[1,1024]{1,0:T(1,128)S(1)} %bitcast.7), channel_id=1, source_target_pairs={{1,0},{2,1},{3,2},{4,3},{5,4},{6,5},{7,6},{9,8},{10,9},{11,10},{12... | collective-permute-start | bytes 12296 | tf_op jit(solution)/shard_map/ppermute | solution.py:222
  10.6 6.6 %collective-permute-start.2 = (f32[8,128]{1,0:T(8,128)S(1)}, f32[8,128]{1,0:T(8,128)S(1)}, u32[]{:S(2)}, u32[]{:S(2)}) collective-permute-start(f32[8,128]{1,0:T(8,128)S(1)} %edges.1), channel_id=1, source_target_pairs={{0,16},{8,24},{16,0},{24,8},{1,17},{9,25},{17,1},{25,9},{2,18},{10... | collective-permute-start | bytes 12296 | tf_op jit(solution)/shard_map/ppermute | solution.py:208
  17.3 3.6 %collective-permute-start.3 = (f32[8,128]{1,0:T(8,128)S(1)}, f32[8,128]{1,0:T(8,128)S(1)}, u32[]{:S(2)}, u32[]{:S(2)}) collective-permute-start(f32[8,128]{1,0:T(8,128)S(1)} %add.12), channel_id=1, source_target_pairs={{0,8},{8,0},{16,24},{24,16},{1,9},{9,1},{17,25},{25,17},{2,10},{10... | collective-permute-start | bytes 12296 | tf_op jit(solution)/shard_map/ppermute | solution.py:208
  20.9 4.8 %collective-permute-start.4 = (f32[8,128]{1,0:T(8,128)S(1)}, f32[8,128]{1,0:T(8,128)S(1)}, u32[]{:S(2)}, u32[]{:S(2)}) collective-permute-start(f32[8,128]{1,0:T(8,128)S(1)} %add.13), channel_id=1, source_target_pairs={{0,4},{1,5},{2,6},{3,7},{4,0},{5,1},{6,2},{7,3},{8,12},{9,13},{10,... | collective-permute-start | bytes 12296 | tf_op jit(solution)/shard_map/ppermute | solution.py:208
  25.7 3.6 %collective-permute-start.5 = (f32[8,128]{1,0:T(8,128)S(1)}, f32[8,128]{1,0:T(8,128)S(1)}, u32[]{:S(2)}, u32[]{:S(2)}) collective-permute-start(f32[8,128]{1,0:T(8,128)S(1)} %add.14), channel_id=1, source_target_pairs={{0,2},{1,3},{2,0},{3,1},{4,6},{5,7},{6,4},{7,5},{8,10},{9,11},{10,... | collective-permute-start | bytes 12296 | tf_op jit(solution)/shard_map/ppermute | solution.py:208
  29.3 1.2 %collective-permute-start.6 = (f32[8,128]{1,0:T(8,128)S(1)}, f32[8,128]{1,0:T(8,128)S(1)}, u32[]{:S(2)}, u32[]{:S(2)}) collective-permute-start(f32[8,128]{1,0:T(8,128)S(1)} %add.15.mine_ref), channel_id=1, source_target_pairs={{0,1},{1,0},{2,3},{3,2},{4,5},{5,4},{6,7},{7,6},{8,9},{9,8},{10,11... | collective-permute-start | bytes 12296 | tf_op jit(solution)/shard_map/ppermute | solution.py:208
